TPU v7x, 512 devices: a whole 4x4x16 slice. The times are simulated.
512 devices in a mesh: prow: 16 (over y, z_hi, core), pcol: 32 (over x, z_lo).
Axes of the slice: x: 4, y: 4, z: 16 (z_hi: 2, z_lo: 8; z = z_hi * 8 + z_lo), core: 2. Of those that a mesh axis runs over, the one named last changes fastest.
Arguments:
- tiles: bfloat16 [16, 32, 16, 256, 256], P('prow', 'pcol'), may hold values from -6 to 6
- tile_ids: int32 [16, 32, 16], P('prow', 'pcol'), may hold values from 0 to 127, as said below
- counts: int32 [16, 32], P('prow', 'pcol'), may hold values from 1 to 16, as said below
- pivots: int32 [256], replicated, may hold values from 0 to 65535, as said below
- l_inverse: bfloat16 [256, 256], P(None, 'pcol'), may hold values from -1 to 1, as said below
- u_inverse: bfloat16 [256, 256], P('prow'), may hold values from -0.125 to 0.5, as said below
Outputs:
- factored: bfloat16 [16, 32, 16, 256, 256], P('prow', 'pcol')
Inputs may be any that keep to these rules, and one draw needn't show every extreme that they name: Live slot s of device (p, q) holds local tile row tile_ids[p, q, s] // 8 and local tile column tile_ids[p, q, s] % 8; live codes of one device are distinct, padded slots hold arbitrary codes. Let R be the tile rows I >= 1 with tile (I, 0) held and C the tile columns J >= 1 with tile (0, J) held. Tile (0, 0) is held; on each prow index R takes the last one to 3 local tile rows, on each pcol index C takes the last one to 3 local tile columns, and both most counts are reached on some index. Every tile whose row is 0 or in R and whose column is 0 or in C is held; no other held tile lies in tile row 0, a tile row of R, or tile column 0. `counts`: some device has 16 live slots. Row r of tile row 0 and row pivots[r] change places; pivots[r] is r or a row of a tile row of R, and the values that differ from their r are distinct. `l_inverse`: lower triangular with unit diagonal. `u_inverse`: upper triangular with a positive diagonal.
All inputs are finite; a program needn't handle non-finite values.
Results may differ from a plain program's by a relative error of at most 0.0056.
Values may be sent and summed in bfloat16 or wider, within the bound.
No kernel may reach another device: no remote copies, remote signals or barrier semaphores. Data moves between devices by JAX's collectives and lax.ppermute only.
A program may use at most 64 MiB of HBM per device.

v0:
```python
import jax
import jax.numpy as jnp
from jax import lax
from jax.sharding import Mesh
from jax.sharding import PartitionSpec as P

TILE_SIDE = 256
LOCAL_ROWS = 16
TILE_SLOTS = 16
LOWER_MOST = 3
UPPER_MOST = 3
HALF_WORK = 4
PCOL = ("pcol_0", "pcol_1")


def laid_out(parts, dim):
    parts = jnp.moveaxis(parts, 0, dim)
    lengths = parts.shape
    return parts.reshape(*lengths[:dim], lengths[dim] * lengths[dim + 1], *lengths[dim + 2 :])


def from_everyone(shard, axis):
    devices = lax.axis_size(axis)
    return lax.all_to_all(
        jnp.broadcast_to(shard[None], (devices, *shard.shape)), axis, 0, 0, tiled=True
    )


def gather_directly(shard, axis, dim):
    return laid_out(from_everyone(shard, axis), dim)


def spread(shard, axes, root):
    shard = jnp.where(lax.axis_index(axes) == root, shard, jnp.zeros_like(shard))
    for axis in axes:
        shard = lax.psum(shard, axis)
    return shard


def from_partner(block, axis, bit):
    count = lax.axis_size(axis)
    route = []
    for low in range(count):
        high = low | 1 << bit
        if high != low and high < count:
            route += [(low, high), (high, low)]
    return lax.ppermute(block, axis, route)


def pick_rows(tile, rows):
    return tile[rows]


def body(tiles, tile_ids, counts, pivots, l_inverse, u_inverse):
    row_count = lax.axis_size("prow")
    col_count = lax.axis_size(PCOL)
    my_row = lax.axis_index("prow")
    my_col = lax.axis_index(PCOL)
    grid_cols = LOCAL_ROWS * row_count // col_count
    total_rows = LOCAL_ROWS * row_count * TILE_SIDE
    local = tiles[0, 0]
    codes = tile_ids[0, 0]
    slot_range = jnp.arange(TILE_SLOTS, dtype=jnp.int32)
    alive = slot_range < counts[0, 0]
    loc_row = codes // grid_cols
    loc_col = codes % grid_cols
    glob_row = my_row + row_count * loc_row
    glob_col = my_col + col_count * loc_col
    col_range = jnp.arange(grid_cols, dtype=jnp.int32)
    upper_inv = lax.all_gather(u_inverse, "prow", axis=0, tiled=True)
    lower_inv = gather_directly(l_inverse, PCOL, 1)
    source_tile = pivots // TILE_SIDE
    source_row = pivots % TILE_SIDE
    gathered = local[:, source_row, :]
    owned = (source_tile[None, :] == glob_row[:, None]) & alive[:, None]
    contrib = jnp.where(owned[:, :, None], gathered, jnp.zeros_like(gathered))
    col_hot = ((loc_col[:, None] == col_range[None, :]) & alive[:, None]).astype(jnp.bfloat16)
    top_flag = (glob_row == 0).astype(jnp.bfloat16)
    top_hot = col_hot * top_flag[:, None]
    flag_part = jnp.sum(
        top_hot.astype(jnp.float32) * (glob_col >= 1).astype(jnp.float32)[:, None], axis=0
    )
    list_size = UPPER_MOST + 1
    rows_used = (glob_row == 0) | jnp.any(owned, axis=1)
    col_mask = jnp.any(
        (loc_col[:, None] == col_range[None, :]) & (alive & rows_used)[:, None], axis=0
    )
    listed = jnp.argsort(jnp.where(col_mask, 0, 1), stable=True)[:list_size]
    list_valid = col_mask[listed]
    list_hot = (
        (loc_col[:, None] == listed[None, :]) & list_valid[None, :] & alive[:, None]
    ).astype(jnp.bfloat16)
    new_part = jnp.einsum("sk,srb->krb", list_hot, contrib, preferred_element_type=jnp.float32)
    old_part = jnp.einsum(
        "sk,srb->krb", list_hot * top_flag[:, None], local, preferred_element_type=jnp.float32
    )
    id_part = jnp.where(list_valid & (my_row == 0), listed + 1, 0).astype(jnp.float32)
    new_sum, old_sum, flag_sum, id_sum = (
        lax.psum(new_part.astype(jnp.bfloat16), "prow").astype(jnp.float32),
        lax.psum(old_part.astype(jnp.bfloat16), "prow").astype(jnp.float32),
        lax.psum(flag_part.astype(jnp.bfloat16), "prow").astype(jnp.float32),
        lax.psum(id_part.astype(jnp.bfloat16), "prow").astype(jnp.float32),
    )
    list_ids = (id_sum + 0.5).astype(jnp.int32) - 1
    back_hot = ((list_ids[:, None] == col_range[None, :]) & (id_sum > 0.5)[:, None]).astype(
        jnp.bfloat16
    )
    new_top = jnp.einsum(
        "kj,krb->jrb", back_hot, new_sum.astype(jnp.bfloat16), preferred_element_type=jnp.float32
    ).astype(jnp.bfloat16)
    old_top = jnp.einsum(
        "kj,krb->jrb", back_hot, old_sum.astype(jnp.bfloat16), preferred_element_type=jnp.float32
    ).astype(jnp.bfloat16)
    anchor_top = (
        jnp.full((total_rows,), -1, jnp.int32)
        .at[pivots]
        .set(jnp.arange(TILE_SIDE, dtype=jnp.int32))
    )
    row_index = glob_row[:, None] * TILE_SIDE + jnp.arange(TILE_SIDE, dtype=jnp.int32)[None, :]
    anchor = anchor_top[row_index]
    moved = (anchor >= 0) & (glob_row >= 1)[:, None]
    from_top = jax.vmap(pick_rows)(old_top[loc_col], jnp.maximum(anchor, 0))
    swapped = jnp.where(moved[:, :, None], from_top, local)
    primed = jnp.where((glob_row == 0)[:, None, None], new_top[loc_col], swapped)
    panel_mask = alive & (glob_col == 0) & (glob_row >= 1)
    panel_slots = jnp.argsort(jnp.where(panel_mask, 0, 1), stable=True)[:LOWER_MOST]
    panel_valid = panel_mask[panel_slots]
    lower_full = jnp.einsum(
        "kab,bc->kac", primed[panel_slots], upper_inv, preferred_element_type=jnp.float32
    )
    lower_list = jnp.where(panel_valid[:, None, None], lower_full, 0.0).astype(jnp.bfloat16)
    lower_rows = jnp.where(panel_valid, loc_row[panel_slots], -1)
    got_list, got_rows = (spread(lower_list, PCOL, 0), spread(lower_rows, PCOL, 0))
    row_match = got_rows[None, :] == loc_row[:, None]
    lower_pick = jnp.sum(
        jnp.where(row_match, jnp.arange(LOWER_MOST, dtype=jnp.int32)[None, :], 0), axis=1
    )
    lower_present = jnp.any(row_match, axis=1)
    column_flags = flag_sum > 0.5
    column_order = jnp.argsort(jnp.where(column_flags, 0, 1), stable=True)[:UPPER_MOST]
    upper_valid = column_flags[column_order]
    upper_full = jnp.einsum(
        "ab,kbc->kac", lower_inv, new_top[column_order], preferred_element_type=jnp.float32
    )
    upper_list = jnp.where(upper_valid[:, None, None], upper_full, 0.0).astype(jnp.bfloat16)
    upper_ids = jnp.where(upper_valid, column_order, -1)
    col_match = upper_ids[None, :] == loc_col[:, None]
    upper_pick = jnp.sum(
        jnp.where(col_match, jnp.arange(UPPER_MOST, dtype=jnp.int32)[None, :], 0), axis=1
    )
    upper_present = jnp.any(col_match, axis=1)
    result = jnp.where(alive[:, None, None], primed, jnp.zeros_like(primed))
    upper_mask = alive & (glob_row == 0) & (glob_col >= 1)
    result = jnp.where(upper_mask[:, None, None], upper_list[upper_pick], result)
    result = result.at[panel_slots].set(
        jnp.where(panel_valid[:, None, None], lower_list, result[panel_slots])
    )
    needs = alive & (glob_row >= 1) & (glob_col >= 1) & lower_present & upper_present
    order = jnp.argsort(jnp.where(needs, 0, 1), stable=True)
    needed = jnp.sum(needs.astype(jnp.int32))

    def trailing(current, lower_tile, upper_index):
        product = jnp.dot(lower_tile, upper_list[upper_index], preferred_element_type=jnp.float32)
        return (current.astype(jnp.float32) - product).astype(jnp.bfloat16)

    half_index = jnp.arange(HALF_WORK, dtype=jnp.int32)
    odd_slots = order[2 * half_index + 1]
    sent_count = needed // 2
    partner_bit = row_count.bit_length() - 2
    got_tiles, got_lower, got_pick, got_count = from_partner(
        (primed[odd_slots], got_list[lower_pick[odd_slots]], upper_pick[odd_slots], sent_count),
        "prow",
        partner_bit,
    )

    def remote_step(position, held):
        value = trailing(got_tiles[position], got_lower[position], got_pick[position])
        return held.at[position].set(value)

    finished = lax.fori_loop(0, got_count, remote_step, jnp.zeros_like(got_tiles))
    returned = from_partner(finished, "prow", partner_bit)

    def even_step(position, held):
        slot = order[2 * position]
        value = trailing(primed[slot], got_list[lower_pick[slot]], upper_pick[slot])
        return held.at[slot].set(value)

    result = lax.fori_loop(0, (needed + 1) // 2, even_step, result)
    sent_live = half_index < sent_count
    result = result.at[odd_slots].set(
        jnp.where(sent_live[:, None, None], returned, result[odd_slots])
    )
    return result[None, None]


def solution(mesh):
    torus = Mesh(mesh.devices.reshape(mesh.shape["prow"], 4, 8), ("prow", "pcol_0", "pcol_1"))
    placed = (
        P("prow", PCOL, None, None, None),
        P("prow", PCOL, None),
        P("prow", PCOL),
        P(),
        P(None, PCOL),
        P("prow", None),
    )
    return jax.shard_map(
        body,
        mesh=torus,
        in_specs=placed,
        out_specs=P("prow", PCOL, None, None, None),
        check_vma=False,
    )
```

profile of v0, /device:TPU:484, one launch (start us, length us, event | category | flops | bytes accessed | tf_op | source)
XLA Modules:
  0.0 684.1 jit_solution(12001899202512432619)
XLA Ops:
  7.9 12.5 %all-to-all-start = ((bf16[32,256,8]{1,2,0:T(8,128)(2,1)}), bf16[32,256,8]{1,2,0:T(8,128)(2,1)S(1)}, u32[]{:S(2)}, u32[]{:S(2)}) async-start(bf16[32,256,8]{1,2,0:T(8,128)(2,1)} %broadcast_in_dim.201), calls=%async_computation | async-start | bytes 262144 | tf_op jit(solution)/shard_map/all_to_all | solution.py:24
  25.0 4.1 copy.83
  29.1 3.8 gather_fusion.2
  32.9 2.1 convolution_convert_fusion.2
  35.0 2.2 fusion.20
  37.4 61.9 %all-reduce = (bf16[4]{0:T(256)(128)(2,1)S(1)}, bf16[8]{0:T(256)(128)(2,1)S(1)}) all-reduce(bf16[4]{0:T(256)(128)(2,1)S(1)} %get-tuple-element.249, bf16[8]{0:T(256)(128)(2,1)S(1)} %multiply_reduce_fusion), channel_id=1, replica_groups=mesh['prow'=16,'pcol_0'=4,'pcol_1'=8] {'prow'}, use_global_device_ids=true, to_apply=%region_6.7 | all-reduce | flops 12 | bytes 48 | tf_op jit(solution)/shard_map/psum | solution.py:102
  103.7 6.4 psum.60
  110.2 9.6 %psum.61 = s32[3]{0:T(128)S(1)} all-reduce(s32[3]{0:T(128)S(1)} %psum.60), channel_id=1, replica_groups=mesh['prow'=16,'pcol_0'=4,'pcol_1'=8] {'pcol_1'}, use_global_device_ids=true, to_apply=%region_14.15 | all-reduce | flops 3 | bytes 24 | tf_op jit(solution)/shard_map/psum | solution.py:36
  122.1 23.0 %gather_fusion.6 = s32[4096]{0:T(1024)S(1)} fusion(s32[65536]{0:T(1024)S(1)} %scatter_custom_fusion, s32[4096]{0:T(1024)S(1)} %broadcast_clamp_fusion), kind=kCustom, calls=%fused_computation.6 | custom fusion | bytes 49152 | tf_op jit(solution)/shard_map/gather | solution.py:120
  145.5 46.9 %all_gather.3 = bf16[256,256]{1,0:T(8,128)(2,1)S(1)} all-gather(bf16[16,256]{1,0:T(8,128)(2,1)S(1)} %copy-done.9), channel_id=1, replica_groups=mesh['prow'=16,'pcol_0'=4,'pcol_1'=8] {'prow'}, dimensions={0}, use_global_device_ids=true | all-gather | bytes 139264 | tf_op jit(solution)/shard_map/all_gather | solution.py:70
  192.5 108.3 %all-reduce.10.cloned.1.call-done = (bf16[4,256,256]{2,0,1:T(4,128)(2,1)}, bf16[4,256,256]{2,0,1:T(4,128)(2,1)}) async-done(((bf16[4,256,256]{2,0,1:T(4,128)(2,1)}, bf16[4,256,256]{2,0,1:T(4,128)(2,1)}), (bf16[4,256,256]{2,0,1:T(4,128)(2,1)}, bf16[4,256,256]{2,0,1:T(4,128)(2,1)})) %all-reduce.10.cloned.1.call-update) | async-done | bytes 1048592 | tf_op jit(solution)/shard_map/psum | solution.py:99
  304.9 2.0 gather_fusion.5
  309.1 40.7 %gather_fusion.18 = bf16[4096,256]{1,0:T(8,128)(2,1)} fusion(bf16[16,256,256]{2,1,0:T(8,128)(2,1)S(1)} %gather_fusion.7, s32[4096]{0:T(1024)S(1)} %bitcast.154), kind=kCustom, calls=%fused_computation.18 | custom fusion | bytes 4227072 | tf_op jit(solution)/shard_map/vmap()/gather | solution.py:51
  349.8 2.0 gather_fusion.4
  351.8 16.1 %copy_select_fusion = (bf16[16,256,256]{2,0,1:T(8,128)(2,1)}, bf16[16,256,256]{2,0,1:T(8,128)(2,1)S(1)}) fusion(bf16[16,256,256]{2,1,0:T(8,128)(2,1)} %gather_fusion.4, pred[16]{0:T(512)(128)(4,1)S(1)} %iota_compare_fusion.3, pred[16]{0:T(512)(128)(4,1)S(1)} %copy-done.13, bf16[1,1,16,256,256]{4,3,2,1,0:T(8,128)(2,1)S(1)} %copy-done.1, ...), kind=kLoop, calls=%fused_computation.46 | loop fusion | flops 4194304 | bytes 12587056 | tf_op jit(solution)/shard_map/jit(_where)/select_n | solution.py:154
  370.0 2.3 copy.61
  376.2 68.7 %all-reduce.6.cloned.1.call-done = bf16[3,256,256]{2,1,0:T(8,128)(2,1)} async-done(((bf16[3,256,256]{2,1,0:T(8,128)(2,1)}), bf16[3,256,256]{2,1,0:T(8,128)(2,1)}) %all-reduce.6.cloned.1.call-update) | async-done | bytes 393232 | tf_op jit(solution)/shard_map/psum | solution.py:36
  445.6 3.0 gather_fusion.13
  448.5 4.9 collective-permute-start.1
  453.5 117.4 %all-reduce.8.cloned.1.call-done = bf16[3,256,256]{2,1,0:T(8,128)(2,1)} async-done(((bf16[3,256,256]{2,1,0:T(8,128)(2,1)}), bf16[3,256,256]{2,1,0:T(8,128)(2,1)}) %all-reduce.8.cloned.1.call-update) | async-done | bytes 393232 | tf_op jit(solution)/shard_map/psum | solution.py:36
  570.8 2.4 gather_fusion.15
  573.2 4.9 collective-permute-start.2
  581.0 4.1 collective-permute-start
  585.8 4.5 collective-permute-start.3
  593.6 6.5 while.23
  597.6 1.8 fusion.73
  600.1 21.9 %collective-permute-start.4 = (bf16[4,256,256]{2,1,0:T(8,128)(2,1)S(1)}, bf16[4,256,256]{2,1,0:T(8,128)(2,1)}, u32[]{:S(2)}, u32[]{:S(2)}) collective-permute-start(bf16[4,256,256]{2,1,0:T(8,128)(2,1)S(1)} %get-tuple-element.124), channel_id=1, source_target_pairs={{0,256},{256,0},{32,288},{288,32},{64,320},{320,64},{96,352},{352,... | collective-permute-start | bytes 1572872 | tf_op jit(solution)/shard_map/ppermute | solution.py:47
  622.0 50.8 %while.22 = (s32[]{:T(128)}, bf16[16,256,256]{2,1,0:T(8,128)(2,1)S(1)}, s32[]{:T(128)}, s32[16]{0:T(128)S(1)}, bf16[16,256,256]{2,1,0:T(8,128)(2,1)}, /*index=5*...) while((s32[]{:T(128)}, ...), condition=%wide.region_24.25_spmd, body=%wide.region_22.24_spmd.sunk | while | flops 33816608 | bytes 656746 | solution.py:188
  630.4 1.8 fusion.70
  640.5 1.8 fusion.70
  650.7 1.8 fusion.70
  671.0 1.8 fusion.70
  (167 shorter events, 50.8 us)
Async XLA Ops:
  7.9 299.7 %all-to-all-start = ((bf16[32,256,8]{1,2,0:T(8,128)(2,1)}), bf16[32,256,8]{1,2,0:T(8,128)(2,1)S(1)}, u32[]{:S(2)}, u32[]{:S(2)}) async-start(bf16[32,256,8]{1,2,0:T(8,128)(2,1)} %broadcast_in_dim.201), calls=%async_computation | async-start | bytes 262144 | tf_op jit(solution)/shard_map/all_to_all | solution.py:24
  20.4 280.5 %all-reduce.10.cloned.1.call-start = ((), (), s32[]{:S(2)}) async-start(), calls=%async_computation.3 | async-start | bytes 2097152 | tf_op jit(solution)/shard_map/psum | solution.py:99
  29.1 3.9 copy-start
  32.9 2.1 copy-start.4
  37.2 66.5 %copy-start.16 = (s32[1,1,16]{2,1,0:T(1,128)S(1)}, s32[1,1,16]{2,1,0:T(1,128)}, u32[]{:S(2)}) copy-start(s32[1,1,16]{2,1,0:T(1,128)} %param.15) | copy-start | bytes 196
  37.2 407.6 %all-reduce.6.cloned.1.call-start = ((), (), s32[]{:S(2)}) async-start(), calls=%async_computation.1 | async-start | bytes 786432 | tf_op jit(solution)/shard_map/psum | solution.py:36
  101.0 1.3 copy-start.19
  102.4 18.2 %copy-start.10 = (s32[3]{0:T(128)}, s32[3]{0:T(128)S(1)}, u32[]{:S(2)}) copy-start(s32[3]{0:T(128)S(1)} %compare_select_fusion.5) | copy-start | bytes 40
  103.7 16.9 %copy-start.14 = (pred[3]{0:T(512)(128)(4,1)}, pred[3]{0:T(512)(128)(4,1)S(1)}, u32[]{:S(2)}) copy-start(pred[3]{0:T(512)(128)(4,1)S(1)} %gather_fusion.8) | copy-start | bytes 13
  119.8 0.8 copy-start.21
  122.1 23.4 %copy-start.9 = (bf16[16,256]{1,0:T(8,128)(2,1)S(1)}, bf16[16,256]{1,0:T(8,128)(2,1)}, u32[]{:S(2)}) copy-start(bf16[16,256]{1,0:T(8,128)(2,1)} %param.19) | copy-start | bytes 24580
  300.8 1.9 copy-start.6
  306.9 0.7 copy-start.20
  349.8 2.0 copy-start.1
  349.8 2.0 copy-start.12
  349.8 2.0 copy-start.13
  368.6 1.3 copy-start.3
  370.0 2.9 copy-start.15
  372.3 1.9 copy-start.18
  372.3 3.8 copy-start.22
  374.0 204.1 %copy-start.17 = (pred[16]{0:T(512)(128)(4,1)S(1)}, pred[16]{0:T(512)(128)(4,1)}, u32[]{:S(2)}) copy-start(pred[16]{0:T(512)(128)(4,1)} %get-tuple-element.226) | copy-start | bytes 52
  374.1 216.8 %copy-start.11 = (s32[3]{0:T(128)S(1)}, s32[3]{0:T(128)}, u32[]{:S(2)}) copy-start(s32[3]{0:T(128)} %copy-done.10) | copy-start | bytes 40
  374.1 196.8 %all-reduce.8.cloned.1.call-start = ((), (), s32[]{:S(2)}) async-start(), calls=%async_computation.2 | async-start | bytes 786432 | tf_op jit(solution)/shard_map/psum | solution.py:36
  445.5 148.0 %copy-start.8 = (s32[3]{0:T(128)S(1)}, s32[3]{0:T(128)}, u32[]{:S(2)}) copy-start(s32[3]{0:T(128)} %constant.175.clone.1) | copy-start | bytes 40
  448.5 144.2 %collective-permute-start.1 = (bf16[4,256,256]{2,1,0:T(8,128)(2,1)}, bf16[4,256,256]{2,1,0:T(8,128)(2,1)S(1)}, u32[]{:S(2)}, u32[]{:S(2)}) collective-permute-start(bf16[4,256,256]{2,1,0:T(8,128)(2,1)} %gather_fusion.13), channel_id=1, source_target_pairs={{0,256},{256,0},{32,288},{288,32},{64,320},{320,64},{96,352},{352,... | collective-permute-start | bytes 1572872 | tf_op jit(solution)/shard_map/ppermute | solution.py:47
  573.2 20.3 %collective-permute-start.2 = (bf16[4,256,256]{2,1,0:T(8,128)(2,1)}, bf16[4,256,256]{2,1,0:T(8,128)(2,1)}, u32[]{:S(2)}, u32[]{:S(2)}) collective-permute-start(bf16[4,256,256]{2,1,0:T(8,128)(2,1)} %gather_fusion.15), channel_id=1, source_target_pairs={{0,256},{256,0},{32,288},{288,32},{64,320},{320,64},{96,352},{352,... | collective-permute-start | bytes 1572872 | tf_op jit(solution)/shard_map/ppermute | solution.py:47
  581.0 11.5 %collective-permute-start = (s32[]{:T(128)}, s32[]{:T(128)}, u32[]{:S(2)}, u32[]{:S(2)}) collective-permute-start(s32[]{:T(128)} %select_n.307), channel_id=1, source_target_pairs={{0,256},{256,0},{32,288},{288,32},{64,320},{320,64},{96,352},{352,... | collective-permute-start | bytes 20 | tf_op jit(solution)/shard_map/ppermute | solution.py:47
  585.8 7.0 %collective-permute-start.3 = (s32[4]{0:T(128)S(1)}, s32[4]{0:T(128)S(1)}, u32[]{:S(2)}, u32[]{:S(2)}) collective-permute-start(s32[4]{0:T(128)S(1)} %gather_fusion.16), channel_id=1, source_target_pairs={{0,256},{256,0},{32,288},{288,32},{64,320},{320,64},{96,352},{352,... | collective-permute-start | bytes 56 | tf_op jit(solution)/shard_map/ppermute | solution.py:47
  592.5 29.5 %copy-start.7 = (s32[3]{0:T(128)S(1)}, s32[3]{0:T(128)}, u32[]{:S(2)}) copy-start(s32[3]{0:T(128)} %constant.168.clone.1) | copy-start | bytes 40
  592.7 0.8 copy-start.5
  600.1 74.1 %collective-permute-start.4 = (bf16[4,256,256]{2,1,0:T(8,128)(2,1)S(1)}, bf16[4,256,256]{2,1,0:T(8,128)(2,1)}, u32[]{:S(2)}, u32[]{:S(2)}) collective-permute-start(bf16[4,256,256]{2,1,0:T(8,128)(2,1)S(1)} %get-tuple-element.124), channel_id=1, source_target_pairs={{0,256},{256,0},{32,288},{288,32},{64,320},{320,64},{96,352},{352,... | collective-permute-start | bytes 1572872 | tf_op jit(solution)/shard_map/ppermute | solution.py:47
  676.2 1.3 copy-start.2
Sparse Core Ops, SparseCore 0:
  37.3 263.4 all-reduce.9
  374.2 70.6 all-reduce.5
  447.8 123.0 all-reduce.7
where the time goes:
time: 686 us; the launch traced here: 684 us
  waiting for transfers between devices  295 us (43%)
  blocking collectives  125 us (18%)
  local copies, waits for them, and re-layouts  112 us (16%)
  starting transfers between devices  53 us (8%)
  loops' own time  31.5 us (5%)
  other arithmetic  30.9 us (5%)
  matrix products  19.7 us (3%)
  between operations  17.1 us (2%)
    psum x2, waiting for transfers between devices, spread(): shard = lax.psum(shard, axis)  186 us
    psum x1, waiting for transfers between devices, body(): lax.psum(new_part.astype(jnp.bfloat16), 'prow').astype(jnp.float32)  108 us
    psum x1, blocking collectives, body(): lax.psum(id_part.astype(jnp.bfloat16), 'prow').astype(jnp.float32)  61.9 us
    all_gather x1, blocking collectives, body(): upper_inv = lax.all_gather(u_inverse, 'prow', axis=0, tiled=True)  46.9 us
    gather x2, local copies, waits for them, and re-layouts, pick_rows(): return tile[rows]  40.7 us
    ppermute x5, starting transfers between devices, from_partner(): return lax.ppermute(block, axis, route)  40.3 us
    another operation x1, loops' own time, body(): result = lax.fori_loop(0, (needed + 1) // 2, even_step, result)  28.3 us
    gather x1, local copies, waits for them, and re-layouts, body(): anchor = anchor_top[row_index]  23 us
  transfers between devices with their start and end apart: 9, of which 4 were waited for; matrix products, arithmetic and copies ran while one was open for 13% of the time, Pallas kernels for 0%

commit v1 on v0

--- a/solution.py
+++ b/solution.py
@@ -96,7 +96,7 @@
     )
     id_part = jnp.where(list_valid & (my_row == 0), listed + 1, 0).astype(jnp.float32)
     new_sum, old_sum, flag_sum, id_sum = (
-        lax.psum(new_part.astype(jnp.bfloat16), "prow").astype(jnp.float32),
+        jnp.sum(lax.all_gather(new_part.astype(jnp.bfloat16), "prow"), axis=0).astype(jnp.float32),
         lax.psum(old_part.astype(jnp.bfloat16), "prow").astype(jnp.float32),
         lax.psum(flag_part.astype(jnp.bfloat16), "prow").astype(jnp.float32),
         lax.psum(id_part.astype(jnp.bfloat16), "prow").astype(jnp.float32),

time: 686 us -> 785 us (1.14)
  waiting for transfers between devices: 295 us -> 387 us
  other arithmetic: 30.9 us -> 39.4 us
    all_gather x0 -> x1, waiting for transfers between devices: none -> 139 us  [body(): lax.all_gather(new_part.astype(jnp.bfloat16), 'prow')]
    psum x1, waiting for transfers between devices: 108 us -> 77.1 us  [body(): lax.psum(old_part.astype(jnp.bfloat16), 'prow').astype(jnp.float32)]
    psum x2, waiting for transfers between devices: 186 us -> 171 us  [spread(): shard = lax.psum(shard, axis)]
  transfers between devices with their start and end apart: 9 -> 10, of which waited for: 4 -> 4; matrix products, arithmetic and copies ran while one was open for 13% -> 16% of each run, Pallas kernels for 0% -> 0%
where the time goes in v1:
time: 785 us; the launch traced here: 784 us
  waiting for transfers between devices  387 us (49%)
  blocking collectives  123 us (16%)
  local copies, waits for them, and re-layouts  109 us (14%)
  starting transfers between devices  55.8 us (7%)
  other arithmetic  39.4 us (5%)
  loops' own time  31.8 us (4%)
  matrix products  19.5 us (2%)
  between operations  18 us (2%)
    psum x2, waiting for transfers between devices, spread(): shard = lax.psum(shard, axis)  171 us
    all_gather x1, waiting for transfers between devices, body(): lax.all_gather(new_part.astype(jnp.bfloat16), 'prow')  139 us
    psum x1, waiting for transfers between devices, body(): lax.psum(old_part.astype(jnp.bfloat16), 'prow').astype(jnp.float32)  77.1 us
    psum x1, blocking collectives, body(): lax.psum(id_part.astype(jnp.bfloat16), 'prow').astype(jnp.float32)  60.1 us
    all_gather x1, blocking collectives, body(): upper_inv = lax.all_gather(u_inverse, 'prow', axis=0, tiled=True)  48.4 us
    ppermute x5, starting transfers between devices, from_partner(): return lax.ppermute(block, axis, route)  43.2 us
    gather x2, local copies, waits for them, and re-layouts, pick_rows(): return tile[rows]  40.7 us
    another operation x1, loops' own time, body(): result = lax.fori_loop(0, (needed + 1) // 2, even_step, result)  28.8 us
  transfers between devices with their start and end apart: 10, of which 4 were waited for; matrix products, arithmetic and copies ran while one was open for 16% of the time, Pallas kernels for 0%

profile of v1, /device:TPU:484, one launch (start us, length us, event | category | flops | bytes accessed | tf_op | source)
XLA Modules:
  0.0 783.9 jit_solution(6393618883489537406)
XLA Ops:
  11.3 3.8 convolution_convert_fusion.2
  15.1 2.5 copy.127
  17.6 2.3 gather_fusion.2
  25.5 12.5 %all-to-all-start = ((bf16[32,256,8]{1,2,0:T(8,128)(2,1)}), bf16[32,256,8]{1,2,0:T(8,128)(2,1)S(1)}, u32[]{:S(2)}, u32[]{:S(2)}) async-start(bf16[32,256,8]{1,2,0:T(8,128)(2,1)} %broadcast_in_dim.201), calls=%async_computation | async-start | bytes 262144 | tf_op jit(solution)/shard_map/all_to_all | solution.py:24
  38.1 6.4 psum.52
  44.6 60.1 %all-reduce = (bf16[4]{0:T(256)(128)(2,1)S(1)}, bf16[8]{0:T(256)(128)(2,1)S(1)}) all-reduce(bf16[4]{0:T(256)(128)(2,1)S(1)} %get-tuple-element.279, bf16[8]{0:T(256)(128)(2,1)S(1)} %multiply_reduce_fusion), channel_id=1, replica_groups=mesh['prow'=16,'pcol_0'=4,'pcol_1'=8] {'prow'}, use_global_device_ids=true, to_apply=%region_6.7 | all-reduce | flops 12 | bytes 48 | tf_op jit(solution)/shard_map/psum | solution.py:102
  104.7 8.3 %psum.53 = s32[3]{0:T(128)S(1)} all-reduce(s32[3]{0:T(128)S(1)} %psum.52), channel_id=1, replica_groups=mesh['prow'=16,'pcol_0'=4,'pcol_1'=8] {'pcol_1'}, use_global_device_ids=true, to_apply=%region_14.15 | all-reduce | flops 3 | bytes 24 | tf_op jit(solution)/shard_map/psum | solution.py:36
  117.0 23.0 %gather_fusion.6 = s32[4096]{0:T(1024)S(1)} fusion(s32[65536]{0:T(1024)S(1)} %scatter_custom_fusion, s32[4096]{0:T(1024)S(1)} %broadcast_clamp_fusion), kind=kCustom, calls=%fused_computation.6 | custom fusion | bytes 49152 | tf_op jit(solution)/shard_map/gather | solution.py:120
  140.9 48.4 %all_gather.11 = bf16[256,256]{1,0:T(8,128)(2,1)} all-gather(bf16[16,256]{1,0:T(8,128)(2,1)S(1)} %copy-done.8), channel_id=1, replica_groups=mesh['prow'=16,'pcol_0'=4,'pcol_1'=8] {'prow'}, dimensions={0}, use_global_device_ids=true | all-gather | bytes 139264 | tf_op jit(solution)/shard_map/all_gather | solution.py:70
  190.6 77.1 %all-reduce.5.cloned.1.call-done = bf16[4,256,256]{2,0,1:T(4,128)(2,1)} async-done(((bf16[4,256,256]{2,0,1:T(4,128)(2,1)}), bf16[4,256,256]{2,0,1:T(4,128)(2,1)}) %all-reduce.5.cloned.1.call-update) | async-done | bytes 524304 | tf_op jit(solution)/shard_map/psum | solution.py:100
  270.2 40.7 %gather_fusion.18 = bf16[4096,256]{1,0:T(8,128)(2,1)} fusion(bf16[16,256,256]{2,1,0:T(8,128)(2,1)S(1)} %gather_fusion.7, s32[4096]{0:T(1024)S(1)} %bitcast.154), kind=kCustom, calls=%fused_computation.18 | custom fusion | bytes 4227072 | tf_op jit(solution)/shard_map/vmap()/gather | solution.py:51
  310.9 139.2 %all-gather.3.cloned.1.call-done = bf16[64,256,256]{2,1,0:T(8,128)(2,1)} async-done(((bf16[4,256,256]{2,1,0:T(8,128)(2,1)}), bf16[64,256,256]{2,1,0:T(8,128)(2,1)}) %all-gather.3.cloned.1.call-update) | async-done | bytes 8388624 | tf_op jit(solution)/shard_map/all_gather | solution.py:99
  450.1 5.0 reduce_sum.51
  456.6 2.0 gather_fusion.5
  459.1 2.3 gather_fusion.4
  461.4 16.0 %copy_select_fusion = (bf16[16,256,256]{2,0,1:T(8,128)(2,1)}, bf16[16,256,256]{2,0,1:T(8,128)(2,1)S(1)}) fusion(bf16[16,256,256]{2,1,0:T(8,128)(2,1)} %gather_fusion.4, pred[16]{0:T(512)(128)(4,1)S(1)} %iota_compare_fusion.3, pred[16]{0:T(512)(128)(4,1)S(1)} %copy-done.14, bf16[1,1,16,256,256]{4,3,2,1,0:T(8,128)(2,1)S(1)} %copy-done.1, ...), kind=kLoop, calls=%fused_computation.46 | loop fusion | flops 4194304 | bytes 12587056 | tf_op jit(solution)/shard_map/jit(_where)/select_n | solution.py:154
  479.5 2.3 copy.103
  485.8 53.6 %all-reduce.7.cloned.1.call-done = bf16[3,256,256]{2,1,0:T(8,128)(2,1)} async-done(((bf16[3,256,256]{2,1,0:T(8,128)(2,1)}), bf16[3,256,256]{2,1,0:T(8,128)(2,1)}) %all-reduce.7.cloned.1.call-update) | async-done | bytes 393232 | tf_op jit(solution)/shard_map/psum | solution.py:36
  540.7 2.2 gather_fusion.13
  542.9 4.9 collective-permute-start.1
  547.8 117.4 %all-reduce.9.cloned.1.call-done = bf16[3,256,256]{2,1,0:T(8,128)(2,1)} async-done(((bf16[3,256,256]{2,1,0:T(8,128)(2,1)}), bf16[3,256,256]{2,1,0:T(8,128)(2,1)}) %all-reduce.9.cloned.1.call-update) | async-done | bytes 393232 | tf_op jit(solution)/shard_map/psum | solution.py:36
  665.2 2.5 gather_fusion.15
  667.7 4.9 collective-permute-start.2
  676.7 3.7 collective-permute-start
  681.6 4.9 collective-permute-start.3
  689.7 7.5 while.23
  697.2 24.7 %collective-permute-start.4 = (bf16[4,256,256]{2,1,0:T(8,128)(2,1)S(1)}, bf16[4,256,256]{2,1,0:T(8,128)(2,1)}, u32[]{:S(2)}, u32[]{:S(2)}) collective-permute-start(bf16[4,256,256]{2,1,0:T(8,128)(2,1)S(1)} %get-tuple-element.124), channel_id=1, source_target_pairs={{0,256},{256,0},{32,288},{288,32},{64,320},{320,64},{96,352},{352,... | collective-permute-start | bytes 1572872 | tf_op jit(solution)/shard_map/ppermute | solution.py:47
  721.9 51.5 %while.22 = (s32[]{:T(128)}, bf16[16,256,256]{2,1,0:T(8,128)(2,1)S(1)}, s32[]{:T(128)}, s32[16]{0:T(128)S(1)}, bf16[16,256,256]{2,1,0:T(8,128)(2,1)}, /*index=5*...) while((s32[]{:T(128)}, ...), condition=%wide.region_24.25_spmd, body=%wide.region_22.24_spmd.sunk | while | flops 33816608 | bytes 656746 | solution.py:188
  730.4 1.8 fusion.70
  740.7 1.8 fusion.70
  761.3 1.8 fusion.70
  771.6 1.8 fusion.70
  (170 shorter events, 56.0 us)
Async XLA Ops:
  6.5 8.6 %copy-start = (bf16[1,1,16,256,256]{4,3,2,1,0:T(8,128)(2,1)S(1)}, bf16[1,1,16,256,256]{4,3,2,1,0:T(8,128)(2,1)}, u32[]{:S(2)}) copy-start(bf16[1,1,16,256,256]{4,3,2,1,0:T(8,128)(2,1)} %param.14) | copy-start | bytes 6291460
  6.5 261.1 %all-reduce.5.cloned.1.call-start = ((), (), s32[]{:S(2)}) async-start(), calls=%async_computation.1 | async-start | bytes 1048576 | tf_op jit(solution)/shard_map/psum | solution.py:100
  15.1 435.1 %all-gather.3.cloned.1.call-start = ((), (), s32[]{:S(2)}) async-start(), calls=%async_computation.4 | async-start | bytes 8912896 | tf_op jit(solution)/shard_map/all_gather | solution.py:99
  21.3 3.5 copy-start.9
  23.6 91.8 %copy-start.10 = (s32[3]{0:T(128)}, s32[3]{0:T(128)S(1)}, u32[]{:S(2)}) copy-start(s32[3]{0:T(128)S(1)} %compare_select_fusion.5) | copy-start | bytes 40
  24.8 90.5 %copy-start.15 = (pred[3]{0:T(512)(128)(4,1)}, pred[3]{0:T(512)(128)(4,1)S(1)}, u32[]{:S(2)}) copy-start(pred[3]{0:T(512)(128)(4,1)S(1)} %gather_fusion.8) | copy-start | bytes 13
  25.5 433.1 %all-to-all-start = ((bf16[32,256,8]{1,2,0:T(8,128)(2,1)}), bf16[32,256,8]{1,2,0:T(8,128)(2,1)S(1)}, u32[]{:S(2)}, u32[]{:S(2)}) async-start(bf16[32,256,8]{1,2,0:T(8,128)(2,1)} %broadcast_in_dim.201), calls=%async_computation | async-start | bytes 262144 | tf_op jit(solution)/shard_map/all_to_all | solution.py:24
  38.0 501.4 %all-reduce.7.cloned.1.call-start = ((), (), s32[]{:S(2)}) async-start(), calls=%async_computation.2 | async-start | bytes 786432 | tf_op jit(solution)/shard_map/psum | solution.py:36
  112.9 4.0 copy-start.20
  116.9 23.9 %copy-start.8 = (bf16[16,256]{1,0:T(8,128)(2,1)S(1)}, bf16[16,256]{1,0:T(8,128)(2,1)}, u32[]{:S(2)}) copy-start(bf16[16,256]{1,0:T(8,128)(2,1)} %param.19) | copy-start | bytes 24580
  116.9 73.6 %copy-start.17 = (s32[1,1,16]{2,1,0:T(1,128)S(1)}, s32[1,1,16]{2,1,0:T(1,128)}, u32[]{:S(2)}) copy-start(s32[1,1,16]{2,1,0:T(1,128)} %param.15) | copy-start | bytes 196
  459.1 2.3 copy-start.1
  459.1 2.3 copy-start.4
  459.1 2.3 copy-start.13
  459.1 2.3 copy-start.14
  478.2 1.3 copy-start.3
  479.5 3.0 copy-start.5
  479.5 3.0 copy-start.16
  481.8 1.9 copy-start.18
  481.8 1.9 copy-start.19
  481.9 3.8 copy-start.21
  483.6 181.6 %all-reduce.9.cloned.1.call-start = ((), (), s32[]{:S(2)}) async-start(), calls=%async_computation.3 | async-start | bytes 786432 | tf_op jit(solution)/shard_map/psum | solution.py:36
  485.8 54.3 %copy-start.11 = (s32[4]{0:T(128)}, s32[4]{0:T(128)S(1)}, u32[]{:S(2)}) copy-start(s32[4]{0:T(128)S(1)} %fusion.48) | copy-start | bytes 52
  539.4 148.4 %copy-start.7 = (s32[1024]{0:T(1024)}, s32[1024]{0:T(1024)S(1)}, u32[]{:S(2)}) copy-start(s32[1024]{0:T(1024)S(1)} %pad_clamp_fusion.1) | copy-start | bytes 12292
  542.9 146.8 %collective-permute-start.1 = (bf16[4,256,256]{2,1,0:T(8,128)(2,1)S(1)}, bf16[4,256,256]{2,1,0:T(8,128)(2,1)S(1)}, u32[]{:S(2)}, u32[]{:S(2)}) collective-permute-start(bf16[4,256,256]{2,1,0:T(8,128)(2,1)S(1)} %gather_fusion.13), channel_id=1, source_target_pairs={{0,256},{256,0},{32,288},{288,32},{64,320},{320,64},{96,352},{352,... | collective-permute-start | bytes 1572872 | tf_op jit(solution)/shard_map/ppermute | solution.py:47
  667.7 21.9 %collective-permute-start.2 = (bf16[4,256,256]{2,1,0:T(8,128)(2,1)}, bf16[4,256,256]{2,1,0:T(8,128)(2,1)}, u32[]{:S(2)}, u32[]{:S(2)}) collective-permute-start(bf16[4,256,256]{2,1,0:T(8,128)(2,1)} %gather_fusion.15), channel_id=1, source_target_pairs={{0,256},{256,0},{32,288},{288,32},{64,320},{320,64},{96,352},{352,... | collective-permute-start | bytes 1572872 | tf_op jit(solution)/shard_map/ppermute | solution.py:47
  676.7 12.9 %collective-permute-start = (s32[]{:T(128)}, s32[]{:T(128)}, u32[]{:S(2)}, u32[]{:S(2)}) collective-permute-start(s32[]{:T(128)} %select_n.307), channel_id=1, source_target_pairs={{0,256},{256,0},{32,288},{288,32},{64,320},{320,64},{96,352},{352,... | collective-permute-start | bytes 20 | tf_op jit(solution)/shard_map/ppermute | solution.py:47
  681.6 8.0 %collective-permute-start.3 = (s32[4]{0:T(128)}, s32[4]{0:T(128)}, u32[]{:S(2)}, u32[]{:S(2)}) collective-permute-start(s32[4]{0:T(128)} %gather_fusion.16), channel_id=1, source_target_pairs={{0,256},{256,0},{32,288},{288,32},{64,320},{320,64},{96,352},{352,... | collective-permute-start | bytes 56 | tf_op jit(solution)/shard_map/ppermute | solution.py:47
  689.6 32.3 %copy-start.6 = (s32[3]{0:T(128)S(1)}, s32[3]{0:T(128)}, u32[]{:S(2)}) copy-start(s32[3]{0:T(128)} %constant.169.clone.1) | copy-start | bytes 40
  697.2 77.0 %collective-permute-start.4 = (bf16[4,256,256]{2,1,0:T(8,128)(2,1)S(1)}, bf16[4,256,256]{2,1,0:T(8,128)(2,1)}, u32[]{:S(2)}, u32[]{:S(2)}) collective-permute-start(bf16[4,256,256]{2,1,0:T(8,128)(2,1)S(1)} %get-tuple-element.124), channel_id=1, source_target_pairs={{0,256},{256,0},{32,288},{288,32},{64,320},{320,64},{96,352},{352,... | collective-permute-start | bytes 1572872 | tf_op jit(solution)/shard_map/ppermute | solution.py:47
  773.4 1.9 copy-start.12
  776.0 1.3 copy-start.2
Sparse Core Ops, SparseCore 0:
  15.2 252.4 all-reduce.4
  270.9 179.1 all-gather.2
  483.8 55.5 all-reduce.6
  542.2 123.0 all-reduce.8
